TPU v7x, 32 devices: a whole 2x2x4 slice. The times are simulated.
32 devices in a mesh: blk: 8 (over z, x), ga: 4 (over y, core).
Axes of the slice: x: 2, y: 2, z: 4, core: 2. Of those that a mesh axis runs over, the one named last changes fastest.
Arguments:
- pair_val: bfloat16 [16, 16, 16, 2048], P('blk', None, None, 'ga'), may hold values from -0.125 to 0.125
- pair_con: bfloat16 [16, 16, 16, 2048], P('blk', None, None, 'ga'), may hold values from -6 to 6
- screened: bfloat16 [16, 2048, 2048], P('blk', None, 'ga'), may hold values from -0.125 to 0.125
- amplitude: bfloat16 [16, 16], P('blk'), may hold values from -6 to 6
- qmap: int32 [16, 16], P('blk'), may hold values from 0 to 15, as said below
Outputs:
- kernel_x: float32 [16, 16], P('blk')
Inputs may be any that keep to these rules, and one draw needn't show every extreme that they name: qmap[k, k'] is the label of the difference k - k' (periodic) on a grid of 8 by 2 points, with the points and the differences labelled at random; every row and every column holds each label once.
All inputs are finite; a program needn't handle non-finite values.
Results may differ from a plain program's by a relative error of at most 0.004.
Values may be sent and summed in bfloat16 or wider, within the bound.
No kernel may reach another device: no remote copies, remote signals or barrier semaphores. Data moves between devices by JAX's collectives and lax.ppermute only.
A program may use at most 64 MiB of HBM per device.

v0:
```python
import jax
import jax.numpy as jnp
from jax import lax
from jax.sharding import PartitionSpec as P

NV = 4
NC = 4


def inverse_rows(qmap):
    total = qmap.shape[1]
    labels = jnp.arange(total, dtype=jnp.int32)
    hits = (qmap[:, :, None] == labels[None, None, :]).astype(jnp.int32)
    return jnp.sum(hits * labels[None, :, None], axis=1)


def swap(value, axis, size, step):
    return lax.ppermute(value, axis, [(i, i ^ step) for i in range(size)])


def body_of(blk, ga):

    def body(pair_val, pair_con, screened, amplitude, qmap):
        local_k, total, band_pairs, width = pair_val.shape
        local_q = screened.shape[0]
        slot = lax.axis_index("ga")
        every_amp = lax.all_gather(amplitude, "blk", axis=0, tiled=True)
        partner = inverse_rows(qmap)
        con_sorted = jnp.take_along_axis(pair_con, partner[:, :, None, None], axis=1)
        con_sorted, every_amp = lax.optimization_barrier((con_sorted, every_amp))
        con_in = lax.all_to_all(con_sorted, "blk", split_axis=1, concat_axis=0, tiled=True)
        val_sorted = jnp.take_along_axis(pair_val, partner[:, :, None, None], axis=1)
        amp_sorted = every_amp[partner].reshape(local_k, total, NV, NC)
        val_five = val_sorted.reshape(local_k, total, NV, NV, width)
        zeta = jnp.einsum(
            "kqavg,kqvc->kqacg", val_five, amp_sorted, preferred_element_type=jnp.float32
        )
        zeta = zeta.astype(jnp.bfloat16).reshape(local_k, total, NV * NC, width)
        far = swap(con_in, "ga", ga, ga // 2)
        near = swap(con_in, "ga", ga, 1)
        zeta_in = lax.all_to_all(zeta, "blk", split_axis=1, concat_axis=0, tiled=True)
        pieces = {0: con_in, 1: near, ga // 2: far, ga // 2 + 1: swap(far, "ga", ga, 1)}
        weights = screened.reshape(local_q, ga, width, screened.shape[2])
        unit = 0.0
        for key, held in pieces.items():
            block = lax.dynamic_index_in_dim(weights, slot ^ key, 1, keepdims=False)
            unit = unit + jnp.einsum(
                "kqxg,qgh->kqxh", held, block, preferred_element_type=jnp.float32
            )
        unit = unit.astype(jnp.bfloat16).reshape(total, local_q, NC, NC, -1)
        zeta = zeta_in.reshape(total, local_q, NV, NC, -1)
        terms = jnp.einsum("kqcyg,kqayg->kac", unit, zeta, preferred_element_type=jnp.float32)
        terms = terms.reshape(blk, 1, local_k, NV * NC)
        terms = jnp.broadcast_to(terms, (blk, ga, local_k, NV * NC)).reshape(
            blk * ga, local_k, NV * NC
        )
        back = lax.all_to_all(terms, ("blk", "ga"), split_axis=0, concat_axis=0, tiled=True)
        return jnp.sum(back, 0) / total

    return body


def solution(mesh):
    placed = (
        P("blk", None, None, "ga"),
        P("blk", None, None, "ga"),
        P("blk", None, "ga"),
        P("blk", None),
        P("blk", None),
    )
    return jax.shard_map(
        body_of(mesh.shape["blk"], mesh.shape["ga"]),
        mesh=mesh,
        in_specs=placed,
        out_specs=P("blk", None),
        check_vma=False,
    )
```

profile of v0, /device:TPU:0, one launch (start us, length us, event | category | flops | bytes accessed | tf_op | source)
XLA Modules:
  0.0 74.7 jit_solution(2706167675406388047)
XLA Ops:
  0.0 0.0 copy-start
  0.0 0.8 %select_reduce_fusion = s32[2,16]{1,0:T(2,128)S(1)} fusion(s32[2,16]{1,0:T(2,128)} %param.11), kind=kLoop, calls=%fused_computation.24 | loop fusion | flops 1504 | bytes 256 | tf_op jit(solution)/shard_map/reduce_sum | solution.py:14
  0.9 0.1 reshape.99
  0.9 0.1 copy-done
  1.1 0.6 gather_fusion.2
  1.7 1.7 %gather_fusion.1 = bf16[32,16,512]{2,1,0:T(8,128)(2,1)S(1)} fusion(bf16[2,16,16,512]{3,2,1,0:T(8,128)(2,1)} %param.8, s32[32]{0:T(128)S(1)} %reshape.99), kind=kCustom, calls=%fused_computation.clone | custom fusion | bytes 1048832 | tf_op jit(solution)/shard_map/jit(take_along_axis)/gather | solution.py:29
  3.4 22.4 %all-gather = bf16[8,2,16]{2,1,0:T(2,128)(2,1)S(1)} all-gather(bf16[1,2,16]{2,1,0:T(2,128)(2,1)} %bitcast.98), channel_id=1, replica_groups=mesh['blk'=8,'ga'=4] {'blk'}, dimensions={0}, use_global_device_ids=true | all-gather | bytes 576 | tf_op jit(solution)/shard_map/all_gather | solution.py:27
  25.8 0.2 broadcast_select_fusion
  26.0 0.8 %copy.96 = bf16[2,16,16,512]{3,2,0,1:T(8,128)(2,1)} copy(bf16[2,16,16,512]{3,2,1,0:T(8,128)(2,1)S(1)} %get-tuple-element.9) | data formatting | bytes 1048576 | tf_op jit(solution)/shard_map/optimization_barrier | solution.py:30
  26.8 3.5 %all-to-all-start.1 = ((bf16[2,16,16,512]{3,2,0,1:T(8,128)(2,1)}), bf16[2,16,16,512]{3,2,0,1:T(8,128)(2,1)S(1)}, u32[]{:S(2)}, u32[]{:S(2)}) async-start(bf16[2,16,16,512]{3,2,0,1:T(8,128)(2,1)} %copy.96), calls=%async_computation.1 | async-start | bytes 1048576 | tf_op jit(solution)/shard_map/all_to_all | solution.py:31
  30.3 0.1 reshape.78
  30.4 0.6 gather_fusion
  31.0 0.1 copy.90
  31.1 0.1 reshape.56
  31.1 0.1 copy.107
  31.3 0.1 reshape.57
  31.4 0.4 fusion.2
  31.8 0.1 reshape.58
  32.0 0.8 %copy.92 = bf16[2,16,16,512]{3,2,0,1:T(8,128)(2,1)} copy(bf16[2,16,16,512]{3,2,1,0:T(8,128)(2,1)S(1)} %reshape.58) | data formatting | bytes 1048576 | tf_op jit(solution)/shard_map/reshape | solution.py:38
  32.8 8.4 %all-to-all-done.1 = bf16[2,16,16,512]{3,2,0,1:T(8,128)(2,1)S(1)} async-done(((bf16[2,16,16,512]{3,2,0,1:T(8,128)(2,1)}), bf16[2,16,16,512]{3,2,0,1:T(8,128)(2,1)S(1)}, u32[]{:S(2)}, u32[]{:S(2)}) %all-to-all-start.1) | async-done | bytes 524320 | tf_op jit(solution)/shard_map/all_to_all | solution.py:31
  41.2 3.7 %all-to-all-start = ((bf16[2,16,16,512]{3,2,0,1:T(8,128)(2,1)}), bf16[2,16,16,512]{3,2,0,1:T(8,128)(2,1)S(1)}, u32[]{:S(2)}, u32[]{:S(2)}) async-start(bf16[2,16,16,512]{3,2,0,1:T(8,128)(2,1)} %copy.92), calls=%async_computation | async-start | bytes 1048576 | tf_op jit(solution)/shard_map/all_to_all | solution.py:41
  45.0 1.6 %collective-permute-start.1 = (bf16[16,2,16,512]{3,2,0,1:T(8,128)(2,1)S(1)}, bf16[16,2,16,512]{3,2,0,1:T(8,128)(2,1)S(1)}, u32[]{:S(2)}, u32[]{:S(2)}) collective-permute-start(bf16[16,2,16,512]{3,2,0,1:T(8,128)(2,1)S(1)} %bitcast.92), channel_id=1, source_target_pairs={{0,2},{1,3},{2,0},{3,1},{4,6},{5,7},{6,4},{7,5},{8,10},{9,11},{10,... | collective-permute-start | bytes 1572872 | tf_op jit(solution)/shard_map/ppermute | solution.py:18
  46.5 0.0 collective-permute-start
  46.5 10.8 %all-to-all-done = bf16[2,16,16,512]{3,2,0,1:T(8,128)(2,1)S(1)} async-done(((bf16[2,16,16,512]{3,2,0,1:T(8,128)(2,1)}), bf16[2,16,16,512]{3,2,0,1:T(8,128)(2,1)S(1)}, u32[]{:S(2)}, u32[]{:S(2)}) %all-to-all-start) | async-done | bytes 524320 | tf_op jit(solution)/shard_map/all_to_all | solution.py:41
  57.3 0.5 copy.94
  57.9 0.0 copy-start.1
  57.9 1.8 %fusion.6 = f32[2,512,16,16]{1,3,2,0:T(8,128)S(1)} fusion(bf16[16,2,16,512]{3,2,0,1:T(8,128)(2,1)S(1)} %bitcast.94, bf16[2,4,512,512]{3,2,1,0:T(8,128)(2,1)} %bitcast.99, s32[]{:T(128)S(6)} %select_n.30), kind=kOutput, calls=%fused_computation.14 | convolution fusion | flops 268435456 | bytes 2621444 | tf_op jit(solution)/shard_map/kqxg,qgh->kqxh/dot_general | solution.py:47
  59.7 0.0 collective-permute-done.1
  59.7 0.1 collective-permute-start.2
  59.8 0.0 collective-permute-done
  59.8 0.6 copy-done.1
  60.4 0.4 convolution_add_fusion.2
  60.9 0.5 convolution_add_fusion.1
  61.3 0.4 collective-permute-done.2
  61.7 0.4 fusion.1
  62.2 0.1 reshape.61
  62.3 0.9 %convolution_bitcast_fusion = f32[16,4,4]{2,1,0:T(4,128)S(1)} fusion(bf16[16,2,4,4,512]{4,3,2,0,1:T(4,128)(2,1)S(1)} %reshape.61, bf16[16,2,4,4,512]{4,1,3,2,0:T(2,128)(2,1)S(1)} %bitcast.95), kind=kOutput, calls=%fused_computation.10 | convolution fusion | flops 2097152 | bytes 1049600 | tf_op jit(solution)/shard_map/kqcyg,kqayg->kac/dot_general | solution.py:52
  63.2 0.1 broadcast_in_dim.22
  63.3 10.8 %all_to_all.38 = f32[32,2,16]{2,1,0:T(2,128)S(1)} all-to-all(f32[32,2,16]{2,1,0:T(2,128)S(1)} %copy.105), channel_id=1, replica_groups=mesh['blk'=8,'ga'=4] {'blk','ga'}, dimensions={0} | all-to-all | bytes 8192 | tf_op jit(solution)/shard_map/all_to_all | solution.py:57
  74.2 0.6 broadcast_multiply_fusion
  (8 shorter events, 0.1 us)
Async XLA Ops:
  0.0 1.1 %copy-start = (bf16[2,16,16,512]{3,2,1,0:T(8,128)(2,1)S(1)}, bf16[2,16,16,512]{3,2,1,0:T(8,128)(2,1)}, u32[]{:S(2)}) copy-start(bf16[2,16,16,512]{3,2,1,0:T(8,128)(2,1)} %param.7) | copy-start | bytes 1572868
  26.8 14.4 %all-to-all-start.1 = ((bf16[2,16,16,512]{3,2,0,1:T(8,128)(2,1)}), bf16[2,16,16,512]{3,2,0,1:T(8,128)(2,1)S(1)}, u32[]{:S(2)}, u32[]{:S(2)}) async-start(bf16[2,16,16,512]{3,2,0,1:T(8,128)(2,1)} %copy.96), calls=%async_computation.1 | async-start | bytes 1048576 | tf_op jit(solution)/shard_map/all_to_all | solution.py:31
  41.2 16.1 %all-to-all-start = ((bf16[2,16,16,512]{3,2,0,1:T(8,128)(2,1)}), bf16[2,16,16,512]{3,2,0,1:T(8,128)(2,1)S(1)}, u32[]{:S(2)}, u32[]{:S(2)}) async-start(bf16[2,16,16,512]{3,2,0,1:T(8,128)(2,1)} %copy.92), calls=%async_computation | async-start | bytes 1048576 | tf_op jit(solution)/shard_map/all_to_all | solution.py:41
  45.0 14.8 %collective-permute-start.1 = (bf16[16,2,16,512]{3,2,0,1:T(8,128)(2,1)S(1)}, bf16[16,2,16,512]{3,2,0,1:T(8,128)(2,1)S(1)}, u32[]{:S(2)}, u32[]{:S(2)}) collective-permute-start(bf16[16,2,16,512]{3,2,0,1:T(8,128)(2,1)S(1)} %bitcast.92), channel_id=1, source_target_pairs={{0,2},{1,3},{2,0},{3,1},{4,6},{5,7},{6,4},{7,5},{8,10},{9,11},{10,... | collective-permute-start | bytes 1572872 | tf_op jit(solution)/shard_map/ppermute | solution.py:18
  46.5 13.3 %collective-permute-start = (bf16[16,2,16,512]{3,2,0,1:T(8,128)(2,1)S(1)}, bf16[16,2,16,512]{3,2,0,1:T(8,128)(2,1)S(1)}, u32[]{:S(2)}, u32[]{:S(2)}) collective-permute-start(bf16[16,2,16,512]{3,2,0,1:T(8,128)(2,1)S(1)} %bitcast.93), channel_id=1, source_target_pairs={{0,1},{1,0},{2,3},{3,2},{4,5},{5,4},{6,7},{7,6},{8,9},{9,8},{10,11... | collective-permute-start | bytes 1572872 | tf_op jit(solution)/shard_map/ppermute | solution.py:18
  57.9 2.5 %copy-start.1 = (bf16[2,2048,512]{2,1,0:T(8,128)(2,1)S(1)}, bf16[2,2048,512]{2,1,0:T(8,128)(2,1)}, u32[]{:S(2)}) copy-start(bf16[2,2048,512]{2,1,0:T(8,128)(2,1)} %param.9) | copy-start | bytes 12582916
  59.7 2.0 %collective-permute-start.2 = (bf16[16,2,16,512]{3,2,0,1:T(8,128)(2,1)S(1)}, bf16[16,2,16,512]{3,2,0,1:T(8,128)(2,1)S(1)}, u32[]{:S(2)}, u32[]{:S(2)}) collective-permute-start(bf16[16,2,16,512]{3,2,0,1:T(8,128)(2,1)S(1)} %collective-permute-done.1), channel_id=1, source_target_pairs={{0,1},{1,0},{2,3},{3,2},{4,5},{5,4},{6,7},{7,6},{8,9},{9,8},{10,11... | collective-permute-start | bytes 1572872 | tf_op jit(solution)/shard_map/ppermute | solution.py:18
where the time goes:
time: 75.1 us; the launch traced here: 74.7 us
  blocking collectives  33.2 us (44%)
  waiting for transfers between devices  19.6 us (26%)
  starting transfers between devices  8.84 us (12%)
  local copies, waits for them, and re-layouts  6.81 us (9%)
  matrix products  4.45 us (6%)
  other arithmetic  1.62 us (2%)
    all_gather x1, blocking collectives, body(): every_amp = lax.all_gather(amplitude, 'blk', axis=0, tiled=True)  22.4 us
    all_to_all x1, waiting for transfers between devices, body(): lax.all_to_all(zeta, 'blk', split_axis=1, concat_axis=0, tiled=True)  10.8 us
    all_to_all x1, blocking collectives, body(): lax.all_to_all(terms, ('blk', 'ga'), split_axis=0, concat_axis=0, tiled=T...  10.8 us
    all_to_all x1, waiting for transfers between devices, body(): lax.all_to_all(con_sorted, 'blk', split_axis=1, concat_axis=0, tiled=True)  8.4 us
    all_to_all x1, starting transfers between devices, body(): lax.all_to_all(zeta, 'blk', split_axis=1, concat_axis=0, tiled=True)  3.69 us
    all_to_all x1, starting transfers between devices, body(): lax.all_to_all(con_sorted, 'blk', split_axis=1, concat_axis=0, tiled=True)  3.49 us
    dot_general x4, matrix products, body(): jnp.einsum('kqxg,qgh->kqxh', held, block, preferred_element_type=jnp.floa...  3.15 us
    gather x2, local copies, waits for them, and re-layouts, body(): jnp.take_along_axis(pair_con, partner[:, :, None, None], axis=1)  1.75 us
  transfers between devices with their start and end apart: 5, of which 3 were waited for; matrix products, arithmetic and copies ran while one was open for 8% of the time, Pallas kernels for 0%

commit v1 on v0

--- a/solution.py
+++ b/solution.py
@@ -24,7 +24,14 @@
         local_k, total, band_pairs, width = pair_val.shape
         local_q = screened.shape[0]
         slot = lax.axis_index("ga")
-        every_amp = lax.all_gather(amplitude, "blk", axis=0, tiled=True)
+        count = lax.axis_size("blk")
+        right = [(i_2, (i_2 + 1) % count) for i_2 in range(count)]
+        terms_2 = [amplitude]
+        for hop in range(1, count):
+            terms_2 = [lax.ppermute(terms_2[0], "blk", right), *terms_2]
+        whole = jnp.concatenate(terms_2, axis=0)
+        turn = (lax.axis_index("blk") + 1) * terms_2[-1].shape[0]
+        every_amp = jnp.roll(whole, turn, axis=0)
         partner = inverse_rows(qmap)
         con_sorted = jnp.take_along_axis(pair_con, partner[:, :, None, None], axis=1)
         con_sorted, every_amp = lax.optimization_barrier((con_sorted, every_amp))

time: 75.1 us -> 96.1 us (1.28)
  waiting for transfers between devices: 19.6 us -> 56.3 us
  blocking collectives: 33.2 us -> 11.1 us
  starting transfers between devices: 8.84 us -> 15.3 us
    ppermute x0 -> x7, waiting for transfers between devices: none -> 38.8 us  [body(): terms_2 = [lax.ppermute(terms_2[0], 'blk', right), *terms_2]]
    all_gather x1 -> x0, blocking collectives: 22.4 us -> none  [body(): every_amp = lax.all_gather(amplitude, 'blk', axis=0, tiled=True)]
    ppermute x0 -> x7, starting transfers between devices: none -> 3.19 us  [body(): terms_2 = [lax.ppermute(terms_2[0], 'blk', right), *terms_2]]
    all_to_all x1, starting transfers between devices: 3.69 us -> 6.73 us  [body(): lax.all_to_all(zeta, 'blk', split_axis=1, concat_axis=0, tiled=True)]
    all_to_all x1, waiting for transfers between devices: 10.8 us -> 8.38 us  [body(): lax.all_to_all(zeta, 'blk', split_axis=1, concat_axis=0, tiled=True)]
    gather x1, local copies, waits for them, and re-layouts: 0.62 us -> 1.66 us  [body(): jnp.take_along_axis(pair_val, partner[:, :, None, None], axis=1)]
    gather x2, local copies, waits for them, and re-layouts: 1.75 us -> 0.7 us  [body(): jnp.take_along_axis(pair_con, partner[:, :, None, None], axis=1)]
  transfers between devices with their start and end apart: 5 -> 12, of which waited for: 3 -> 10; matrix products, arithmetic and copies ran while one was open for 8% -> 10% of each run, Pallas kernels for 0% -> 0%
where the time goes in v1:
time: 96.1 us; the launch traced here: 95.8 us
  waiting for transfers between devices  56.3 us (59%)
  starting transfers between devices  15.3 us (16%)
  blocking collectives  11.1 us (12%)
  local copies, waits for them, and re-layouts  6.82 us (7%)
  matrix products  4.45 us (5%)
  other arithmetic  1.56 us (2%)
    ppermute x7, waiting for transfers between devices, body(): terms_2 = [lax.ppermute(terms_2[0], 'blk', right), *terms_2]  38.8 us
    all_to_all x1, blocking collectives, body(): lax.all_to_all(terms, ('blk', 'ga'), split_axis=0, concat_axis=0, tiled=T...  11.1 us
    all_to_all x1, waiting for transfers between devices, body(): lax.all_to_all(con_sorted, 'blk', split_axis=1, concat_axis=0, tiled=True)  8.77 us
    all_to_all x1, waiting for transfers between devices, body(): lax.all_to_all(zeta, 'blk', split_axis=1, concat_axis=0, tiled=True)  8.38 us
    all_to_all x1, starting transfers between devices, body(): lax.all_to_all(zeta, 'blk', split_axis=1, concat_axis=0, tiled=True)  6.73 us
    all_to_all x1, starting transfers between devices, body(): lax.all_to_all(con_sorted, 'blk', split_axis=1, concat_axis=0, tiled=True)  3.49 us
    ppermute x7, starting transfers between devices, body(): terms_2 = [lax.ppermute(terms_2[0], 'blk', right), *terms_2]  3.19 us
    dot_general x4, matrix products, body(): jnp.einsum('kqxg,qgh->kqxh', held, block, preferred_element_type=jnp.floa...  3.16 us
  transfers between devices with their start and end apart: 12, of which 10 were waited for; matrix products, arithmetic and copies ran while one was open for 10% of the time, Pallas kernels for 0%

profile of v1, /device:TPU:0, one launch (start us, length us, event | category | flops | bytes accessed | tf_op | source)
XLA Modules:
  0.0 95.8 jit_solution(7993552906717018568)
XLA Ops:
  0.0 0.0 copy-start
  0.0 0.0 copy-start.1
  0.0 3.0 %collective-permute-start = (bf16[2,16]{1,0:T(2,128)(2,1)}, bf16[2,16]{1,0:T(2,128)(2,1)S(1)}, u32[]{:S(2)}, u32[]{:S(2)}) collective-permute-start(bf16[2,16]{1,0:T(2,128)(2,1)} %param.10), channel_id=1, source_target_pairs={{0,4},{4,8},{8,12},{12,16},{16,20},{20,24},{24,28},{28,0},{1,5},{5... | collective-permute-start | bytes 200 | tf_op jit(solution)/shard_map/ppermute | solution.py:31
  3.0 0.8 select_reduce_fusion
  3.8 0.1 reshape.97
  3.8 0.0 copy-done
  3.8 0.6 gather_fusion.1
  4.5 1.7 %gather_fusion.2 = bf16[32,16,512]{2,1,0:T(8,128)(2,1)S(1)} fusion(bf16[2,16,16,512]{3,2,1,0:T(8,128)(2,1)} %param.7, s32[32]{0:T(128)S(1)} %reshape.97), kind=kCustom, calls=%fused_computation.1.clone | custom fusion | bytes 1048832 | tf_op jit(solution)/shard_map/jit(take_along_axis)/gather | solution.py:39
  6.1 0.2 broadcast_select_fusion
  6.3 1.4 %collective-permute-done = bf16[2,16]{1,0:T(2,128)(2,1)S(1)} collective-permute-done((bf16[2,16]{1,0:T(2,128)(2,1)}, bf16[2,16]{1,0:T(2,128)(2,1)S(1)}, u32[]{:S(2)}, u32[]{:S(2)}) %collective-permute-start) | collective-permute-done | bytes 96 | tf_op jit(solution)/shard_map/ppermute | solution.py:31
  7.7 0.2 collective-permute-start.1
  7.9 6.1 %collective-permute-done.1 = bf16[2,16]{1,0:T(2,128)(2,1)S(1)} collective-permute-done((bf16[2,16]{1,0:T(2,128)(2,1)S(1)}, bf16[2,16]{1,0:T(2,128)(2,1)S(1)}, u32[]{:S(2)}, u32[]{:S(2)}) %collective-permute-start.1) | collective-permute-done | bytes 96 | tf_op jit(solution)/shard_map/ppermute | solution.py:31
  14.0 0.0 collective-permute-start.2
  14.0 6.3 %collective-permute-done.2 = bf16[2,16]{1,0:T(2,128)(2,1)S(1)} collective-permute-done((bf16[2,16]{1,0:T(2,128)(2,1)S(1)}, bf16[2,16]{1,0:T(2,128)(2,1)S(1)}, u32[]{:S(2)}, u32[]{:S(2)}) %collective-permute-start.2) | collective-permute-done | bytes 96 | tf_op jit(solution)/shard_map/ppermute | solution.py:31
  20.3 0.0 collective-permute-start.3
  20.3 6.3 %collective-permute-done.3 = bf16[2,16]{1,0:T(2,128)(2,1)S(1)} collective-permute-done((bf16[2,16]{1,0:T(2,128)(2,1)S(1)}, bf16[2,16]{1,0:T(2,128)(2,1)S(1)}, u32[]{:S(2)}, u32[]{:S(2)}) %collective-permute-start.3) | collective-permute-done | bytes 96 | tf_op jit(solution)/shard_map/ppermute | solution.py:31
  26.5 0.0 collective-permute-start.4
  26.5 6.3 %collective-permute-done.4 = bf16[2,16]{1,0:T(2,128)(2,1)S(1)} collective-permute-done((bf16[2,16]{1,0:T(2,128)(2,1)S(1)}, bf16[2,16]{1,0:T(2,128)(2,1)S(1)}, u32[]{:S(2)}, u32[]{:S(2)}) %collective-permute-start.4) | collective-permute-done | bytes 96 | tf_op jit(solution)/shard_map/ppermute | solution.py:31
  32.8 0.0 collective-permute-start.5
  32.8 6.3 %collective-permute-done.5 = bf16[2,16]{1,0:T(2,128)(2,1)S(1)} collective-permute-done((bf16[2,16]{1,0:T(2,128)(2,1)S(1)}, bf16[2,16]{1,0:T(2,128)(2,1)S(1)}, u32[]{:S(2)}, u32[]{:S(2)}) %collective-permute-start.5) | collective-permute-done | bytes 96 | tf_op jit(solution)/shard_map/ppermute | solution.py:31
  39.1 0.0 collective-permute-start.6
  39.1 6.3 %collective-permute-done.6 = bf16[2,16]{1,0:T(2,128)(2,1)S(1)} collective-permute-done((bf16[2,16]{1,0:T(2,128)(2,1)S(1)}, bf16[2,16]{1,0:T(2,128)(2,1)S(1)}, u32[]{:S(2)}, u32[]{:S(2)}) %collective-permute-start.6) | collective-permute-done | bytes 96 | tf_op jit(solution)/shard_map/ppermute | solution.py:31
  45.3 0.0 copy-done.1
  45.3 0.1 concatenate.6
  45.5 0.8 copy.96
  46.3 3.5 %all-to-all-start.1 = ((bf16[2,16,16,512]{3,2,0,1:T(8,128)(2,1)}), bf16[2,16,16,512]{3,2,0,1:T(8,128)(2,1)S(1)}, u32[]{:S(2)}, u32[]{:S(2)}) async-start(bf16[2,16,16,512]{3,2,0,1:T(8,128)(2,1)} %copy.96), calls=%async_computation.1 | async-start | bytes 1048576 | tf_op jit(solution)/shard_map/all_to_all | solution.py:38
  49.8 0.1 reshape.78
  49.9 0.1 reshape.57
  50.0 0.6 gather_fusion
  50.6 0.1 copy.90
  50.7 0.1 reshape.56
  50.8 0.1 copy.107
  50.9 0.4 fusion.2
  51.4 0.1 reshape.58
  51.5 0.8 copy.92
  52.3 8.8 %all-to-all-done.1 = bf16[2,16,16,512]{3,2,0,1:T(8,128)(2,1)S(1)} async-done(((bf16[2,16,16,512]{3,2,0,1:T(8,128)(2,1)}), bf16[2,16,16,512]{3,2,0,1:T(8,128)(2,1)S(1)}, u32[]{:S(2)}, u32[]{:S(2)}) %all-to-all-start.1) | async-done | bytes 524320 | tf_op jit(solution)/shard_map/all_to_all | solution.py:38
  61.1 6.7 %all-to-all-start = ((bf16[2,16,16,512]{3,2,0,1:T(8,128)(2,1)}), bf16[2,16,16,512]{3,2,0,1:T(8,128)(2,1)S(1)}, u32[]{:S(2)}, u32[]{:S(2)}) async-start(bf16[2,16,16,512]{3,2,0,1:T(8,128)(2,1)} %copy.92), calls=%async_computation | async-start | bytes 1048576 | tf_op jit(solution)/shard_map/all_to_all | solution.py:48
  67.9 1.9 %collective-permute-start.8 = (bf16[16,2,16,512]{3,2,0,1:T(8,128)(2,1)S(1)}, bf16[16,2,16,512]{3,2,0,1:T(8,128)(2,1)S(1)}, u32[]{:S(2)}, u32[]{:S(2)}) collective-permute-start(bf16[16,2,16,512]{3,2,0,1:T(8,128)(2,1)S(1)} %bitcast.89), channel_id=1, source_target_pairs={{0,2},{1,3},{2,0},{3,1},{4,6},{5,7},{6,4},{7,5},{8,10},{9,11},{10,... | collective-permute-start | bytes 1572872 | tf_op jit(solution)/shard_map/ppermute | solution.py:18
  69.7 0.0 collective-permute-start.7
  69.7 8.4 %all-to-all-done = bf16[2,16,16,512]{3,2,0,1:T(8,128)(2,1)S(1)} async-done(((bf16[2,16,16,512]{3,2,0,1:T(8,128)(2,1)}), bf16[2,16,16,512]{3,2,0,1:T(8,128)(2,1)S(1)}, u32[]{:S(2)}, u32[]{:S(2)}) %all-to-all-start) | async-done | bytes 524320 | tf_op jit(solution)/shard_map/all_to_all | solution.py:48
  78.1 0.5 copy.94
  78.6 0.0 copy-start.2
  78.7 1.8 %fusion.6 = f32[2,512,16,16]{1,3,2,0:T(8,128)S(1)} fusion(bf16[16,2,16,512]{3,2,0,1:T(8,128)(2,1)S(1)} %bitcast.91, bf16[2,4,512,512]{3,2,1,0:T(8,128)(2,1)} %bitcast.95, s32[]{:T(128)S(6)} %select_n.45), kind=kOutput, calls=%fused_computation.14 | convolution fusion | flops 268435456 | bytes 2621444 | tf_op jit(solution)/shard_map/kqxg,qgh->kqxh/dot_general | solution.py:54
  80.5 0.0 collective-permute-done.8
  80.5 0.1 collective-permute-start.9
  80.6 0.0 collective-permute-done.7
  80.6 0.6 copy-done.2
  81.2 0.4 convolution_add_fusion.2
  81.6 0.5 convolution_add_fusion.1
  82.1 0.4 collective-permute-done.9
  82.5 0.4 fusion.1
  82.9 0.1 reshape.61
  83.0 0.9 convolution_bitcast_fusion
  83.9 0.1 broadcast_in_dim.22
  84.1 11.1 %all_to_all.38 = f32[32,2,16]{2,1,0:T(2,128)S(1)} all-to-all(f32[32,2,16]{2,1,0:T(2,128)S(1)} %copy.105), channel_id=1, replica_groups=mesh['blk'=8,'ga'=4] {'blk','ga'}, dimensions={0} | all-to-all | bytes 8192 | tf_op jit(solution)/shard_map/all_to_all | solution.py:64
  95.2 0.6 broadcast_multiply_fusion
  (9 shorter events, 0.2 us)
Async XLA Ops:
  0.0 3.8 %copy-start = (bf16[2,16,16,512]{3,2,1,0:T(8,128)(2,1)S(1)}, bf16[2,16,16,512]{3,2,1,0:T(8,128)(2,1)}, u32[]{:S(2)}) copy-start(bf16[2,16,16,512]{3,2,1,0:T(8,128)(2,1)} %param.8) | copy-start | bytes 1572868
  0.0 45.3 %copy-start.1 = (bf16[2,16]{1,0:T(2,128)(2,1)S(1)}, bf16[2,16]{1,0:T(2,128)(2,1)}, u32[]{:S(2)}) copy-start(bf16[2,16]{1,0:T(2,128)(2,1)} %param.10) | copy-start | bytes 196
  0.0 7.7 %collective-permute-start = (bf16[2,16]{1,0:T(2,128)(2,1)}, bf16[2,16]{1,0:T(2,128)(2,1)S(1)}, u32[]{:S(2)}, u32[]{:S(2)}) collective-permute-start(bf16[2,16]{1,0:T(2,128)(2,1)} %param.10), channel_id=1, source_target_pairs={{0,4},{4,8},{8,12},{12,16},{16,20},{20,24},{24,28},{28,0},{1,5},{5... | collective-permute-start | bytes 200 | tf_op jit(solution)/shard_map/ppermute | solution.py:31
  7.7 6.3 %collective-permute-start.1 = (bf16[2,16]{1,0:T(2,128)(2,1)S(1)}, bf16[2,16]{1,0:T(2,128)(2,1)S(1)}, u32[]{:S(2)}, u32[]{:S(2)}) collective-permute-start(bf16[2,16]{1,0:T(2,128)(2,1)S(1)} %collective-permute-done), channel_id=1, source_target_pairs={{0,4},{4,8},{8,12},{12,16},{16,20},{20,24},{24,28},{28,0},{1,5},{5... | collective-permute-start | bytes 200 | tf_op jit(solution)/shard_map/ppermute | solution.py:31
  14.0 6.3 %collective-permute-start.2 = (bf16[2,16]{1,0:T(2,128)(2,1)S(1)}, bf16[2,16]{1,0:T(2,128)(2,1)S(1)}, u32[]{:S(2)}, u32[]{:S(2)}) collective-permute-start(bf16[2,16]{1,0:T(2,128)(2,1)S(1)} %collective-permute-done.1), channel_id=1, source_target_pairs={{0,4},{4,8},{8,12},{12,16},{16,20},{20,24},{24,28},{28,0},{1,5},{5... | collective-permute-start | bytes 200 | tf_op jit(solution)/shard_map/ppermute | solution.py:31
  20.3 6.3 %collective-permute-start.3 = (bf16[2,16]{1,0:T(2,128)(2,1)S(1)}, bf16[2,16]{1,0:T(2,128)(2,1)S(1)}, u32[]{:S(2)}, u32[]{:S(2)}) collective-permute-start(bf16[2,16]{1,0:T(2,128)(2,1)S(1)} %collective-permute-done.2), channel_id=1, source_target_pairs={{0,4},{4,8},{8,12},{12,16},{16,20},{20,24},{24,28},{28,0},{1,5},{5... | collective-permute-start | bytes 200 | tf_op jit(solution)/shard_map/ppermute | solution.py:31
  26.5 6.3 %collective-permute-start.4 = (bf16[2,16]{1,0:T(2,128)(2,1)S(1)}, bf16[2,16]{1,0:T(2,128)(2,1)S(1)}, u32[]{:S(2)}, u32[]{:S(2)}) collective-permute-start(bf16[2,16]{1,0:T(2,128)(2,1)S(1)} %collective-permute-done.3), channel_id=1, source_target_pairs={{0,4},{4,8},{8,12},{12,16},{16,20},{20,24},{24,28},{28,0},{1,5},{5... | collective-permute-start | bytes 200 | tf_op jit(solution)/shard_map/ppermute | solution.py:31
  32.8 6.3 %collective-permute-start.5 = (bf16[2,16]{1,0:T(2,128)(2,1)S(1)}, bf16[2,16]{1,0:T(2,128)(2,1)S(1)}, u32[]{:S(2)}, u32[]{:S(2)}) collective-permute-start(bf16[2,16]{1,0:T(2,128)(2,1)S(1)} %collective-permute-done.4), channel_id=1, source_target_pairs={{0,4},{4,8},{8,12},{12,16},{16,20},{20,24},{24,28},{28,0},{1,5},{5... | collective-permute-start | bytes 200 | tf_op jit(solution)/shard_map/ppermute | solution.py:31
  39.1 6.3 %collective-permute-start.6 = (bf16[2,16]{1,0:T(2,128)(2,1)S(1)}, bf16[2,16]{1,0:T(2,128)(2,1)S(1)}, u32[]{:S(2)}, u32[]{:S(2)}) collective-permute-start(bf16[2,16]{1,0:T(2,128)(2,1)S(1)} %collective-permute-done.5), channel_id=1, source_target_pairs={{0,4},{4,8},{8,12},{12,16},{16,20},{20,24},{24,28},{28,0},{1,5},{5... | collective-permute-start | bytes 200 | tf_op jit(solution)/shard_map/ppermute | solution.py:31
  46.3 14.8 %all-to-all-start.1 = ((bf16[2,16,16,512]{3,2,0,1:T(8,128)(2,1)}), bf16[2,16,16,512]{3,2,0,1:T(8,128)(2,1)S(1)}, u32[]{:S(2)}, u32[]{:S(2)}) async-start(bf16[2,16,16,512]{3,2,0,1:T(8,128)(2,1)} %copy.96), calls=%async_computation.1 | async-start | bytes 1048576 | tf_op jit(solution)/shard_map/all_to_all | solution.py:38
  61.1 17.0 %all-to-all-start = ((bf16[2,16,16,512]{3,2,0,1:T(8,128)(2,1)}), bf16[2,16,16,512]{3,2,0,1:T(8,128)(2,1)S(1)}, u32[]{:S(2)}, u32[]{:S(2)}) async-start(bf16[2,16,16,512]{3,2,0,1:T(8,128)(2,1)} %copy.92), calls=%async_computation | async-start | bytes 1048576 | tf_op jit(solution)/shard_map/all_to_all | solution.py:48
  67.9 12.6 %collective-permute-start.8 = (bf16[16,2,16,512]{3,2,0,1:T(8,128)(2,1)S(1)}, bf16[16,2,16,512]{3,2,0,1:T(8,128)(2,1)S(1)}, u32[]{:S(2)}, u32[]{:S(2)}) collective-permute-start(bf16[16,2,16,512]{3,2,0,1:T(8,128)(2,1)S(1)} %bitcast.89), channel_id=1, source_target_pairs={{0,2},{1,3},{2,0},{3,1},{4,6},{5,7},{6,4},{7,5},{8,10},{9,11},{10,... | collective-permute-start | bytes 1572872 | tf_op jit(solution)/shard_map/ppermute | solution.py:18
  69.7 10.9 %collective-permute-start.7 = (bf16[16,2,16,512]{3,2,0,1:T(8,128)(2,1)S(1)}, bf16[16,2,16,512]{3,2,0,1:T(8,128)(2,1)S(1)}, u32[]{:S(2)}, u32[]{:S(2)}) collective-permute-start(bf16[16,2,16,512]{3,2,0,1:T(8,128)(2,1)S(1)} %bitcast.90), channel_id=1, source_target_pairs={{0,1},{1,0},{2,3},{3,2},{4,5},{5,4},{6,7},{7,6},{8,9},{9,8},{10,11... | collective-permute-start | bytes 1572872 | tf_op jit(solution)/shard_map/ppermute | solution.py:18
  78.6 2.5 %copy-start.2 = (bf16[2,2048,512]{2,1,0:T(8,128)(2,1)S(1)}, bf16[2,2048,512]{2,1,0:T(8,128)(2,1)}, u32[]{:S(2)}) copy-start(bf16[2,2048,512]{2,1,0:T(8,128)(2,1)} %param.9) | copy-start | bytes 12582916
  80.5 2.0 %collective-permute-start.9 = (bf16[16,2,16,512]{3,2,0,1:T(8,128)(2,1)S(1)}, bf16[16,2,16,512]{3,2,0,1:T(8,128)(2,1)S(1)}, u32[]{:S(2)}, u32[]{:S(2)}) collective-permute-start(bf16[16,2,16,512]{3,2,0,1:T(8,128)(2,1)S(1)} %collective-permute-done.8), channel_id=1, source_target_pairs={{0,1},{1,0},{2,3},{3,2},{4,5},{5,4},{6,7},{7,6},{8,9},{9,8},{10,11... | collective-permute-start | bytes 1572872 | tf_op jit(solution)/shard_map/ppermute | solution.py:18
